TPU v7x, 256 devices: a whole 4x4x8 slice. The times are simulated.
256 devices in a mesh: row: 32 (over z_hi, x, core), col: 8 (over y, z_lo).
Axes of the slice: x: 4, y: 4, z: 8 (z_hi: 4, z_lo: 2; z = z_hi * 2 + z_lo), core: 2. Of those that a mesh axis runs over, the one named last changes fastest.
Arguments:
- pivots: int32 [256], replicated, may hold values from 0 to 32767, as said below
- panel: float32 [32768, 256], P(('row', 'col')), may hold values from -6 to 6
- prior: bfloat16 [32768, 3072], P(('row', 'col')), may hold values from -0.796875 to 0.796875
- finished: bfloat16 [32768, 256], P(('row', 'col')), may hold values from -6 to 6
- pairs: int32 [32768], replicated, may hold values from 0 to 639999, as said below
- occupied: bfloat16 [800, 120], replicated, may hold values from -0.21875 to 0.21875
Outputs:
- updated: float32 [32768, 256], P(('row', 'col'))
- halves: float32 [256, 120, 800], P(('row', 'col'))
Inputs may be any that keep to these rules, and one draw needn't show every extreme that they name: `pivots`: distinct rows; at most 2 of them lie among the rows of one device (aligned blocks of 128 rows), and one device holds exactly 2. `pairs`: each value a * 800 + b with 0 <= b <= a < 800; all distinct and increasing.
All inputs are finite; a program needn't handle non-finite values.
Results may differ from a plain program's by a relative error of at most 0.0003.
Values may be sent and summed in bfloat16 or wider, within the bound.
A program may use at most 64 MiB of HBM per device.

v0:
```python
import jax
import jax.numpy as jnp
from jax import lax
from jax.sharding import PartitionSpec as P


def half_transform(received, pair_ids, occupied):
    orbitals = occupied.shape[0]
    pair_count = received.shape[0]
    vector_count = received.shape[1]
    first_ao = pair_ids // orbitals
    second_ao = pair_ids % orbitals
    off_diag = first_ao != second_ao
    occ_first = jnp.take(occupied, first_ao, axis=0)
    occ_second = jnp.where(
        off_diag[:, None], jnp.take(occupied, second_ao, axis=0), jnp.zeros((), jnp.bfloat16)
    )
    coeffs = jnp.concatenate([occ_first, occ_second], axis=0)
    targets = jnp.concatenate([second_ao, first_ao], axis=0).astype(jnp.int32)
    entries = jnp.concatenate([received, received], axis=0)
    doubled = 2 * pair_count
    wanted = min(doubled, max(1024, doubled // 8))
    block_rows = wanted
    for candidate in range(wanted, 0, -1):
        if doubled % candidate == 0:
            block_rows = candidate
            break
    columns = jnp.arange(orbitals, dtype=jnp.int32)

    def one_block(block_index, accumulated):
        start = block_index * block_rows
        coeff_block = lax.dynamic_slice_in_dim(coeffs, start, block_rows, 0)
        target_block = lax.dynamic_slice_in_dim(targets, start, block_rows, 0)
        entry_block = lax.dynamic_slice_in_dim(entries, start, block_rows, 0)
        matches = target_block[:, None] == columns[None, :]
        spread = jnp.where(
            matches[None, :, :], entry_block.T[:, :, None], jnp.zeros((), jnp.bfloat16)
        )
        return accumulated + jnp.einsum(
            "pi,vpm->vim", coeff_block, spread, preferred_element_type=jnp.float32
        )

    initial = jnp.zeros((vector_count, occupied.shape[1], orbitals), jnp.float32)
    return lax.fori_loop(0, doubled // block_rows, one_block, initial)


def per_device(pivots, panel, prior, finished, pairs, occupied):
    rows_dev = prior.shape[0]
    row_count = lax.axis_size("row")
    col_count = lax.axis_size("col")
    own_index = lax.axis_index("row") * col_count + lax.axis_index("col")
    owner = pivots // rows_dev
    local_rows = pivots % rows_dev
    owned = owner == own_index
    picked = jnp.take(prior, local_rows, axis=0).astype(jnp.float32)
    contribution = jnp.where(owned[:, None], picked, jnp.zeros_like(picked))
    pivot_rows = lax.psum(contribution, ("row", "col")).astype(jnp.bfloat16)
    updated = panel - lax.dot_general(
        prior, pivot_rows, (((1,), (1,)), ((), ())), preferred_element_type=jnp.float32
    )
    by_device = pairs.reshape(row_count, col_count, rows_dev)
    col_pairs = lax.dynamic_slice_in_dim(by_device, lax.axis_index("col"), 1, 1).reshape(-1)
    grouped = finished.reshape(rows_dev, row_count, finished.shape[1] // row_count)
    received = lax.all_to_all(grouped, "row", split_axis=1, concat_axis=0, tiled=True)
    partials = half_transform(
        received.reshape(received.shape[0], received.shape[2]), col_pairs, occupied
    )
    halves = lax.psum_scatter(partials, "col", scatter_dimension=0, tiled=True)
    return (updated, halves)


def solution(mesh):
    return jax.shard_map(
        per_device,
        mesh=mesh,
        in_specs=(
            P(),
            P(("row", "col"), None),
            P(("row", "col"), None),
            P(("row", "col"), None),
            P(),
            P(),
        ),
        out_specs=(P(("row", "col"), None), P(("row", "col"), None, None)),
        check_vma=False,
    )
```

profile of v0, /device:TPU:1, one launch (start us, length us, event | category | flops | bytes accessed | tf_op | source)
XLA Modules:
  0.0 254.0 jit_solution(17810283203826027613)
XLA Ops:
  7.2 0.0 copy-start
  7.2 0.0 copy-start.1
  7.2 1.7 copy.17
  8.9 12.6 %all-to-all-start = ((bf16[128,32,8]{0,2,1:T(8,128)(2,1)}), bf16[128,32,8]{0,2,1:T(8,128)(2,1)S(1)}, u32[]{:S(2)}, u32[]{:S(2)}) async-start(bf16[128,32,8]{0,2,1:T(8,128)(2,1)} %bitcast.4), calls=%async_computation | async-start | bytes 131072 | tf_op jit(solution)/shard_map/all_to_all | solution.py:64
  21.4 0.0 reduce-scatter.2.cloned.1.call-start
  21.5 1.0 broadcast_remainder_fusion
  22.5 1.0 compare_reduce_fusion
  23.5 0.0 copy-done.1
  23.5 12.1 %gather_fusion.2 = bf16[4096,120]{1,0:T(8,128)(2,1)S(1)} fusion(bf16[800,120]{1,0:T(8,128)(2,1)S(1)} %copy-done.1, s32[4096]{0:T(1024)S(1)} %get-tuple-element.172), kind=kCustom, calls=%fused_computation.1.clone | custom fusion | bytes 1982464 | tf_op jit(solution)/shard_map/jit(_take)/gather | solution.py:16
  35.7 12.1 %gather_fusion.1 = bf16[4096,120]{1,0:T(8,128)(2,1)S(1)} fusion(bf16[800,120]{1,0:T(8,128)(2,1)S(1)} %copy-done.1, s32[4096]{0:T(1024)S(1)} %fusion.21), kind=kCustom, calls=%fused_computation.clone | custom fusion | bytes 1982464 | tf_op jit(solution)/shard_map/jit(_take)/gather | solution.py:14
  47.8 2.1 broadcast_select_fusion
  50.0 1.4 select_select_fusion
  51.4 0.4 pad_maximum_fusion
  51.8 3.0 %copy.18 = bf16[8192,120]{0,1:T(8,128)(2,1)} copy(bf16[8192,120]{1,0:T(8,128)(2,1)S(1)} %pad_maximum_fusion) | data formatting | bytes 3932160
  54.8 0.0 all-to-all-done
  54.8 55.6 %while.14 = (s32[]{:T(128)}, f32[8,120,800]{1,2,0:T(8,128)}, s32[8192]{0:T(1024)S(1)}, bf16[8192,8]{0,1:T(8,128)(2,1)S(1)}, bf16[8192,120]{0,1:T(8,128)(2,1)}, /*index=5*/s32[]{:T(128)}, s32[]{:T(128)}, s32[]{:T(128)}, s32[]{:T(128)}) while((s32[]{:T(128)}, f32[8,120,800]{1,2,0:T(8,128)}, s32[8192]{0:T(1024)S(1)}, ...), condition=%wide.region_2.4_spmd.clone, body=%wide.region_1.3_spmd.clone.sunk | while | flops 1581772800 | bytes 8294561 | solution.py:44
  54.9 0.6 iota_compare_fusion.2
  55.5 5.9 %bitcast_add_fusion.2 = f32[8,120,800]{1,2,0:T(8,128)} fusion(f32[8,120,800]{1,2,0:T(8,128)} %get-tuple-element.216, pred[1024,800]{0,1:T(8,128)(4,1)S(1)} %iota_compare_fusion.2, bf16[8,1024]{1,0:T(8,128)(2,1)S(1)} %dynamic-slice_bitcast_fusion.2, pred[]{:T(512)S(6)} %compare.6, bf16[8192,120]{0,1:T(8,128)(2,1)} %get-tuple-element.228, ...), kind=kOutput, calls=%fused_computation.9.clone.1 | convolution fusion | flops 1580953600 | bytes 7430149 | tf_op jit(solution)/shard_map/while/body/eval_jaxpr/pi,vpm->vim/dot_general | solution.py:39
  61.4 0.6 iota_compare_fusion.2
  62.0 6.4 %bitcast_add_fusion.2 = f32[8,120,800]{1,2,0:T(8,128)} fusion(f32[8,120,800]{1,2,0:T(8,128)} %get-tuple-element.216, pred[1024,800]{0,1:T(8,128)(4,1)S(1)} %iota_compare_fusion.2, bf16[8,1024]{1,0:T(8,128)(2,1)S(1)} %dynamic-slice_bitcast_fusion.2, pred[]{:T(512)S(6)} %compare.6, bf16[8192,120]{0,1:T(8,128)(2,1)} %get-tuple-element.228, ...), kind=kOutput, calls=%fused_computation.9.clone.1 | convolution fusion | flops 1580953600 | bytes 7430149 | tf_op jit(solution)/shard_map/while/body/eval_jaxpr/pi,vpm->vim/dot_general | solution.py:39
  68.4 0.6 iota_compare_fusion.2
  69.0 6.4 %bitcast_add_fusion.2 = f32[8,120,800]{1,2,0:T(8,128)} fusion(f32[8,120,800]{1,2,0:T(8,128)} %get-tuple-element.216, pred[1024,800]{0,1:T(8,128)(4,1)S(1)} %iota_compare_fusion.2, bf16[8,1024]{1,0:T(8,128)(2,1)S(1)} %dynamic-slice_bitcast_fusion.2, pred[]{:T(512)S(6)} %compare.6, bf16[8192,120]{0,1:T(8,128)(2,1)} %get-tuple-element.228, ...), kind=kOutput, calls=%fused_computation.9.clone.1 | convolution fusion | flops 1580953600 | bytes 7430149 | tf_op jit(solution)/shard_map/while/body/eval_jaxpr/pi,vpm->vim/dot_general | solution.py:39
  75.4 0.6 iota_compare_fusion.2
  76.0 6.4 %bitcast_add_fusion.2 = f32[8,120,800]{1,2,0:T(8,128)} fusion(f32[8,120,800]{1,2,0:T(8,128)} %get-tuple-element.216, pred[1024,800]{0,1:T(8,128)(4,1)S(1)} %iota_compare_fusion.2, bf16[8,1024]{1,0:T(8,128)(2,1)S(1)} %dynamic-slice_bitcast_fusion.2, pred[]{:T(512)S(6)} %compare.6, bf16[8192,120]{0,1:T(8,128)(2,1)} %get-tuple-element.228, ...), kind=kOutput, calls=%fused_computation.9.clone.1 | convolution fusion | flops 1580953600 | bytes 7430149 | tf_op jit(solution)/shard_map/while/body/eval_jaxpr/pi,vpm->vim/dot_general | solution.py:39
  82.4 0.6 iota_compare_fusion.2
  83.0 6.4 %bitcast_add_fusion.2 = f32[8,120,800]{1,2,0:T(8,128)} fusion(f32[8,120,800]{1,2,0:T(8,128)} %get-tuple-element.216, pred[1024,800]{0,1:T(8,128)(4,1)S(1)} %iota_compare_fusion.2, bf16[8,1024]{1,0:T(8,128)(2,1)S(1)} %dynamic-slice_bitcast_fusion.2, pred[]{:T(512)S(6)} %compare.6, bf16[8192,120]{0,1:T(8,128)(2,1)} %get-tuple-element.228, ...), kind=kOutput, calls=%fused_computation.9.clone.1 | convolution fusion | flops 1580953600 | bytes 7430149 | tf_op jit(solution)/shard_map/while/body/eval_jaxpr/pi,vpm->vim/dot_general | solution.py:39
  89.4 0.6 iota_compare_fusion.2
  90.1 6.4 %bitcast_add_fusion.2 = f32[8,120,800]{1,2,0:T(8,128)} fusion(f32[8,120,800]{1,2,0:T(8,128)} %get-tuple-element.216, pred[1024,800]{0,1:T(8,128)(4,1)S(1)} %iota_compare_fusion.2, bf16[8,1024]{1,0:T(8,128)(2,1)S(1)} %dynamic-slice_bitcast_fusion.2, pred[]{:T(512)S(6)} %compare.6, bf16[8192,120]{0,1:T(8,128)(2,1)} %get-tuple-element.228, ...), kind=kOutput, calls=%fused_computation.9.clone.1 | convolution fusion | flops 1580953600 | bytes 7430149 | tf_op jit(solution)/shard_map/while/body/eval_jaxpr/pi,vpm->vim/dot_general | solution.py:39
  96.4 0.6 iota_compare_fusion.2
  97.1 6.4 %bitcast_add_fusion.2 = f32[8,120,800]{1,2,0:T(8,128)} fusion(f32[8,120,800]{1,2,0:T(8,128)} %get-tuple-element.216, pred[1024,800]{0,1:T(8,128)(4,1)S(1)} %iota_compare_fusion.2, bf16[8,1024]{1,0:T(8,128)(2,1)S(1)} %dynamic-slice_bitcast_fusion.2, pred[]{:T(512)S(6)} %compare.6, bf16[8192,120]{0,1:T(8,128)(2,1)} %get-tuple-element.228, ...), kind=kOutput, calls=%fused_computation.9.clone.1 | convolution fusion | flops 1580953600 | bytes 7430149 | tf_op jit(solution)/shard_map/while/body/eval_jaxpr/pi,vpm->vim/dot_general | solution.py:39
  103.5 0.6 iota_compare_fusion.2
  104.1 6.4 %bitcast_add_fusion.2 = f32[8,120,800]{1,2,0:T(8,128)} fusion(f32[8,120,800]{1,2,0:T(8,128)} %get-tuple-element.216, pred[1024,800]{0,1:T(8,128)(4,1)S(1)} %iota_compare_fusion.2, bf16[8,1024]{1,0:T(8,128)(2,1)S(1)} %dynamic-slice_bitcast_fusion.2, pred[]{:T(512)S(6)} %compare.6, bf16[8192,120]{0,1:T(8,128)(2,1)} %get-tuple-element.228, ...), kind=kOutput, calls=%fused_computation.9.clone.1 | convolution fusion | flops 1580953600 | bytes 7430149 | tf_op jit(solution)/shard_map/while/body/eval_jaxpr/pi,vpm->vim/dot_general | solution.py:39
  110.5 0.0 copy-start.3
  110.5 0.0 reduce-scatter.2.cloned.1.call-update
  110.5 0.6 copy-done.3
  111.2 0.0 copy-done
  111.2 1.6 gather_fusion
  112.8 0.0 copy-start.2
  112.8 2.4 convert_select_fusion
  115.1 0.0 copy-done.2
  115.1 0.1 copy.16
  115.2 130.6 %all-reduce.1 = bf16[256,3072]{1,0:T(8,128)(2,1)S(1)} all-reduce(f32[256,3072]{1,0:T(8,128)} %convert_select_fusion), channel_id=1, replica_groups=mesh['row'=32,'col'=8] {'row','col'}, use_global_device_ids=true, to_apply=%region_0.1 | all-reduce | flops 786432 | bytes 4718592 | tf_op jit(solution)/shard_map/psum | solution.py:57
  245.8 0.6 fusion.18
  246.4 0.8 copy.19
  247.2 0.0 reduce-scatter.2.cloned.1.call-done
  (25 shorter events, 0.2 us)
Async XLA Ops:
  7.2 104.0 %copy-start = (bf16[128,3072]{1,0:T(8,128)(2,1)S(1)}, bf16[128,3072]{1,0:T(8,128)(2,1)}, u32[]{:S(2)}) copy-start(bf16[128,3072]{1,0:T(8,128)(2,1)} %param.12) | copy-start | bytes 2359300
  7.2 16.4 %copy-start.1 = (bf16[800,120]{1,0:T(8,128)(2,1)S(1)}, bf16[800,120]{1,0:T(8,128)(2,1)}, u32[]{:S(2)}) copy-start(bf16[800,120]{1,0:T(8,128)(2,1)} %param.15) | copy-start | bytes 576004
  8.9 46.0 %all-to-all-start = ((bf16[128,32,8]{0,2,1:T(8,128)(2,1)}), bf16[128,32,8]{0,2,1:T(8,128)(2,1)S(1)}, u32[]{:S(2)}, u32[]{:S(2)}) async-start(bf16[128,32,8]{0,2,1:T(8,128)(2,1)} %bitcast.4), calls=%async_computation | async-start | bytes 131072 | tf_op jit(solution)/shard_map/all_to_all | solution.py:64
  21.4 225.7 %reduce-scatter.2.cloned.1.call-start = ((), (), s32[]{:S(2)}) async-start(), calls=%async_computation.2 | async-start | bytes 3686400 | tf_op jit(solution)/shard_map/reduce_scatter | solution.py:68
  110.5 0.7 copy-start.3
  112.8 2.4 copy-start.2
Sparse Core Ops, SparseCore 0:
  110.6 78.9 reduce-scatter.1
where the time goes:
time: 255 us; the launch traced here: 254 us
  blocking collectives  131 us (51%)
  matrix products  51.2 us (20%)
  local copies, waits for them, and re-layouts  32.1 us (13%)
  between operations  14.2 us (6%)
  other arithmetic  13.1 us (5%)
  starting transfers between devices  12.6 us (5%)
    psum x1, blocking collectives, per_device(): pivot_rows = lax.psum(contribution, ('row', 'col')).astype(jnp.bfloat16)  131 us
    dot_general x8, matrix products, one_block(): jnp.einsum('pi,vpm->vim', coeff_block, spread, preferred_element_type=jnp...  50.6 us
    all_to_all x1, starting transfers between devices, per_device(): lax.all_to_all(grouped, 'row', split_axis=1, concat_axis=0, tiled=True)  12.6 us
    gather x1, local copies, waits for them, and re-layouts, half_transform(): occ_first = jnp.take(occupied, first_ao, axis=0)  12.1 us
    gather x1, local copies, waits for them, and re-layouts, half_transform(): jnp.take(occupied, second_ao, axis=0)  12.1 us
    unnamed x12, local copies, waits for them, and re-layouts  6.15 us
  transfers between devices with their start and end apart: 2, of which 0 were waited for; matrix products, arithmetic and copies ran while one was open for 15% of the time, Pallas kernels for 0%

commit v1 on v0

v1 whole, which is shorter than its diff:
```python
import functools
from collections import namedtuple

import jax
import jax.numpy as jnp
from jax import lax
from jax.experimental import pallas as pl
from jax.experimental.pallas import tpu as pltpu
from jax.sharding import PartitionSpec as P

MESH = pl.DeviceIdType.MESH
BF, F32, I32 = jnp.bfloat16, jnp.float32, jnp.int32
Dims = namedtuple("Dims", ("x", "y", "zh", "zl", "c"))
FULL = Dims(4, 4, 4, 2, 2)

NAO = 800
GROUP = 64
BLOCK = 256
TILE_ROWS = 2912
GROUPS = 46
UNROLL = 8

UNIT_TILES = (4, 4, 4)
UNIT_ORDERS = (("x", "y", "z"), ("y", "z", "x"), ("z", "x", "y"))


def nt(a, b):
    return lax.dot_general(a, b, (((1,), (1,)), ((), ())), preferred_element_type=F32)


def nn(a, b):
    return lax.dot_general(a, b, (((1,), (0,)), ((), ())), preferred_element_type=F32)


def iota(shape, dim):
    return lax.broadcasted_iota(I32, shape, dim)


def log2(n):
    assert n & (n - 1) == 0
    return n.bit_length() - 1


def mod(v, n):
    return v & (n - 1)


def div(v, n):
    return v >> log2(n)


def onehot(cond):
    return jnp.where(cond, 1.0, 0.0).astype(BF)


def coordinates(dims, device):
    col = mod(device, dims.y * dims.zl)
    row = div(device, dims.y * dims.zl)
    core = mod(row, dims.c)
    x = mod(div(row, dims.c), dims.x)
    zh = div(row, dims.c * dims.x)
    return dict(x=x, y=div(col, dims.zl), z=zh * dims.zl + mod(col, dims.zl), c=core)


def mesh_id(dims, p):
    row = (div(p["z"], dims.zl) * dims.x + p["x"]) * dims.c + p["c"]
    col = p["y"] * dims.zl + mod(p["z"], dims.zl)
    return (row, col)


class Plan:
    def __init__(self, dims, k, rows):
        self.dims = dims
        self.size = dict(x=dims.x, y=dims.y, z=dims.zh * dims.zl, c=dims.c)
        self.n = dims.x * dims.y * dims.zh * dims.zl * dims.c
        self.slots = 2 * self.n
        self.kt_half = k // 128 // 2
        self.rows = rows
        self.units = []
        first = 0
        for tiles, order in zip(UNIT_TILES, UNIT_ORDERS):
            self.units.append(
                dict(
                    tiles=tiles,
                    first=first,
                    order=order,
                    r1=-(-4 * tiles // 8) * 8,
                    n=[self.size[a] for a in order],
                )
            )
            first += tiles
        assert first == self.kt_half
        self.plane = dims.x * dims.y
        self.pole = self.size["z"] * dims.c


def move(me, **changes):
    return {**me, **changes}


def comm_kernel(plan, *refs):
    dims, size, n = plan.dims, plan.size, plan.n
    nu = len(plan.units)
    (piv_col, piv_row, prior, finished, out, vectors) = refs[:6]
    scratch = list(refs[6:])
    take = lambda count: [scratch.pop(0) for _ in range(count)]
    first_out = take(nu)
    first_in = take(nu)
    gathered = take(nu)
    (partner_prior, part_out, part_in, a_out, a_in, b_out, b_in) = take(7)
    (send1, recv1, send2, recv2, send3, recv3, send_a, recv_a, send_b, recv_b,
     send_p, recv_p, send_q, recv_q) = take(14)

    own = lax.axis_index("row") * (dims.y * dims.zl) + lax.axis_index("col")
    me = coordinates(dims, own)
    core = me["c"]
    other = move(me, c=1 - core)

    def step(axis, by):
        return mod(me[axis] + by, size[axis])

    lines = []
    for axis in ("x", "y", "z"):
        for by in range(1, size[axis]):
            for c in (core, 1 - core):
                lines.append(move(me, **{axis: step(axis, by), "c": c}))
    plane_peers = []
    for bx in range(dims.x):
        for by in range(dims.y):
            if bx or by:
                plane_peers.append(move(me, x=step("x", bx), y=step("y", by)))
    corners = []
    for bx in range(1, dims.x):
        for by in range(1, dims.y):
            corners.append(move(me, x=step("x", bx), y=step("y", by)))
    pole_peers = []
    for bz in range(size["z"]):
        for c in (core, 1 - core):
            if bz or c is not core:
                pole_peers.append(move(me, z=step("z", bz), c=c))
    peers = lines + corners + [other]

    barrier = pltpu.get_barrier_semaphore()
    for p in peers:
        pl.semaphore_signal(barrier, inc=1, device_id=mesh_id(dims, p), device_id_type=MESH)

    def remote(src, dst, send, recv, p):
        copy = pltpu.make_async_remote_copy(
            src_ref=src, dst_ref=dst, send_sem=send, recv_sem=recv,
            device_id=mesh_id(dims, p), device_id_type=MESH,
        )
        copy.start()

    def wait_bytes(ref, sem):
        pltpu.make_async_copy(ref, ref, sem).wait()

    npiv = piv_col.shape[0]
    here = onehot(piv_col[...] == own * plan.rows + iota((npiv, plan.rows), 1))
    has = nn(jnp.ones((32, npiv), BF), here)
    before = onehot(iota((plan.rows, plan.rows), 0) < iota((plan.rows, plan.rows), 1))
    rank = nn(has.astype(BF), before)
    q = iota((32, plan.rows), 0)
    wanted = (mod(q, 4) - core * 2).astype(F32)
    select = jnp.where((has > 0.5) & (rank == wanted), 1.0, 0.0).astype(BF)
    for h in range(2):
        for u, unit in enumerate(plan.units):
            k0 = (h * plan.kt_half + unit["first"]) * 128
            rows = nn(select, prior[:, k0 : k0 + unit["tiles"] * 128])
            r1 = unit["r1"]
            part = jnp.zeros((r1, 128), F32)
            which = div(iota((r1, 128), 0), 4)
            for kt in range(unit["tiles"]):
                part = jnp.where(which == kt, rows[:r1, kt * 128 : (kt + 1) * 128], part)
            first_out[u][h] = part.astype(BF)
    for u, unit in enumerate(plan.units):
        first_in[u][me[unit["order"][0]] * dims.c + core] = first_out[u][core]

    r = iota((n, n), 0)
    v = coordinates(dims, iota((n, n), 1))
    spot = ((v["x"] * dims.y + v["y"]) * size["z"] + v["z"]) * dims.c + v["c"]
    a_rows = nt(onehot(r == spot), finished[...]).astype(BF)
    for i in range(plan.plane):
        a_out[i] = a_rows[i * plan.pole : (i + 1) * plan.pole]
    my_plane = me["x"] * dims.y + me["y"]
    my_pole = me["z"] * dims.c + core
    a_in[my_plane] = a_out[my_plane]

    pl.semaphore_wait(barrier, len(peers))

    for p in plane_peers:
        remote(a_out.at[p["x"] * dims.y + p["y"]], a_in.at[my_plane], send_a, recv_a, p)
    for u, unit in enumerate(plan.units):
        axis = unit["order"][0]
        for by in range(size[axis]):
            for c in (core, 1 - core):
                if by or c is not core:
                    remote(
                        first_out[u].at[c], first_in[u].at[me[axis] * dims.c + core],
                        send1.at[u], recv1.at[u], move(me, **{axis: step(axis, by), "c": c}),
                    )
    half = plan.kt_half * 128
    remote(
        prior.at[:, pl.ds(pl.multiple_of((1 - core) * half, half), half)],
        partner_prior, send_p, recv_p, other,
    )

    wait_bytes(a_in.at[pl.ds(0, plan.plane - 1)], recv_a)
    mixed = a_in[...].reshape(n, plan.rows)
    source = mod(r, plan.plane) * plan.pole + div(r, plan.plane)
    b_rows = nn(onehot(iota((n, n), 1) == source), mixed).astype(BF)
    for i in range(plan.pole):
        b_out[i] = b_rows[i * plan.plane : (i + 1) * plan.plane]
    b_in[my_pole] = b_out[my_pole]
    for p in pole_peers:
        remote(b_out.at[p["z"] * dims.c + p["c"]], b_in.at[my_pole], send_b, recv_b, p)

    sends2 = []
    for u, unit in enumerate(plan.units):
        n1, n2, n3 = unit["n"]
        a1, a2, a3 = unit["order"]
        r1, tiles = unit["r1"], unit["tiles"]
        wait_bytes(first_in[u].at[pl.ds(0, n1 * dims.c - 1)], recv1.at[u])
        got = first_in[u][...].reshape(n1 * dims.c * r1, 128)
        shape = (tiles * n1 * 4, n1 * dims.c * r1)
        ro, ci = iota(shape, 0), iota(shape, 1)
        kt, slot = div(ro, n1 * 4), mod(ro, 4)
        target = (mod(div(ro, 4), n1) * dims.c + div(slot, 2)) * r1 + kt * 4 + slot
        rows = nn(onehot(ci == target), got).astype(BF)
        base = pl.multiple_of((me[a3] * n2 + me[a2]) * (n1 * 4), n1 * 4)
        for t in range(tiles):
            gathered[u][t, pl.ds(base, n1 * 4)] = rows[t * n1 * 4 : (t + 1) * n1 * 4]
        block = gathered[u].at[:, pl.ds(base, n1 * 4)]
        for by in range(1, n2):
            remote(block, block, send2.at[u], recv2.at[u], move(me, **{a2: step(a2, by)}))
        sends2.append((n1 * 4) * (n2 - 1))

    for u, unit in enumerate(plan.units):
        n1, n2, n3 = unit["n"]
        a3 = unit["order"][2]
        wait_bytes(gathered[u].at[:, pl.ds(0, sends2[u])], recv2.at[u])
        base = pl.multiple_of(me[a3] * (n2 * n1 * 4), n2 * n1 * 4)
        block = gathered[u].at[:, pl.ds(base, n2 * n1 * 4)]
        for by in range(1, n3):
            remote(block, block, send3.at[u], recv3.at[u], move(me, **{a3: step(a3, by)}))

    wait_bytes(b_in.at[pl.ds(0, plan.pole - 1)], recv_b)
    mixed = b_in[...].reshape(n, plan.rows)
    w = coordinates(dims, r)
    source = (w["z"] * dims.c + w["c"]) * plan.plane + w["x"] * dims.y + w["y"]
    vectors[...] = nn(onehot(iota((n, n), 1) == source), mixed)

    owner_c = div(piv_col[...], plan.rows)
    owner_r = div(piv_row[...], plan.rows)
    lower = onehot((owner_c == owner_r) & (piv_row[...] < piv_col[...]))
    place = nn(lower, jnp.ones((npiv, 128), BF)).astype(I32)
    o = coordinates(dims, jnp.broadcast_to(owner_c, (npiv, 128)))

    wait_bytes(partner_prior, recv_p)
    mine = jnp.zeros((plan.rows, npiv), F32)
    theirs = jnp.zeros((plan.rows, npiv), F32)
    for u, unit in enumerate(plan.units):
        n1, n2, n3 = unit["n"]
        a1, a2, a3 = unit["order"]
        wait_bytes(gathered[u].at[:, pl.ds(0, n2 * n1 * 4 * (n3 - 1))], recv3.at[u])
        line = ((o[a3] * n2 + o[a2]) * n1 + o[a1]) * 4 + o["c"] * 2 + place
        pick = jnp.concatenate(
            [onehot(iota((npiv, 128), 1) + s == line) for s in range(0, plan.slots, 128)], axis=1
        )
        if plan.slots < 128:
            pick = pick[:, : plan.slots]
        for t in range(unit["tiles"]):
            rows = nn(pick, gathered[u][t]).astype(BF)
            k0 = (unit["first"] + t) * 128
            mine += nt(prior[:, pl.ds(pl.multiple_of(core * half + k0, 128), 128)], rows)
            theirs += nt(partner_prior[:, k0 : k0 + 128], rows)
    part_out[...] = theirs
    remote(part_out, part_in, send_q, recv_q, other)

    for u, unit in enumerate(plan.units):
        n1, n2, n3 = unit["n"]
        wait_bytes(first_in[u].at[pl.ds(0, n1 * dims.c - 1)], send1.at[u])
        wait_bytes(gathered[u].at[:, pl.ds(0, sends2[u])], send2.at[u])
        wait_bytes(gathered[u].at[:, pl.ds(0, n2 * n1 * 4 * (n3 - 1))], send3.at[u])
    wait_bytes(a_in.at[pl.ds(0, plan.plane - 1)], send_a)
    wait_bytes(b_in.at[pl.ds(0, plan.pole - 1)], send_b)
    wait_bytes(partner_prior, send_p)
    wait_bytes(part_in, recv_q)
    wait_bytes(part_out, send_q)
    out[...] = mine + part_in[...]


def communicate(plan, pivots, prior, finished):
    npiv = pivots.shape[0]
    vmem = pl.BlockSpec(memory_space=pltpu.VMEM)
    dma = pltpu.SemaphoreType.DMA
    nu = len(plan.units)
    n, rows = plan.n, plan.rows
    scratch = [pltpu.VMEM((2, u["r1"], 128), BF) for u in plan.units]
    scratch += [pltpu.VMEM((u["n"][0] * plan.dims.c, u["r1"], 128), BF) for u in plan.units]
    scratch += [pltpu.VMEM((u["tiles"], plan.slots, 128), BF) for u in plan.units]
    scratch += [
        pltpu.VMEM((rows, plan.kt_half * 128), BF),
        pltpu.VMEM((rows, npiv), F32),
        pltpu.VMEM((rows, npiv), F32),
        pltpu.VMEM((plan.plane, plan.pole, rows), BF),
        pltpu.VMEM((plan.plane, plan.pole, rows), BF),
        pltpu.VMEM((plan.pole, plan.plane, rows), BF),
        pltpu.VMEM((plan.pole, plan.plane, rows), BF),
    ]
    scratch += [dma((nu,))] * 6 + [dma] * 8
    return pl.pallas_call(
        functools.partial(comm_kernel, plan),
        out_shape=(
            jax.ShapeDtypeStruct((rows, npiv), F32),
            jax.ShapeDtypeStruct((n, rows), F32),
        ),
        in_specs=[vmem] * 4,
        out_specs=(vmem, vmem),
        scratch_shapes=scratch,
        compiler_params=pltpu.CompilerParams(
            collective_id=0, has_side_effects=True, vmem_limit_bytes=40 * 1024 * 1024
        ),
        name="exchange",
    )(pivots.reshape(npiv, 1), pivots.reshape(1, npiv), prior, finished)


def group_of(pair):
    first = pair // NAO
    second = pair % NAO
    block = first >> 7
    return (block * (block + 1) * 64 + (first & 127) * (block + 1) + (second >> 7)) >> log2(GROUP)


def half_kernel(last, pairs, vector, occ_t, out, lane, line, tiles, dense, seq_g, seq_b):
    blocks = last.shape[0]
    steps = GROUPS + blocks - 1
    total = -(-steps // UNROLL) * UNROLL

    def schedule(t, state):
        g, b = state
        seq_g[t] = g
        seq_b[t] = b
        leave = (group_of(last[b]) > g) | (b == blocks - 1)
        return jnp.where(leave, g + 1, g), jnp.where(leave, b, b + 1)

    lax.fori_loop(0, total, schedule, (jnp.int32(0), jnp.int32(0)))

    flat = pairs[...].astype(F32)
    first = jnp.floor((flat + 0.5) * (1.0 / NAO)).astype(I32)
    second = pairs[...] - first * NAO
    row_block = first >> 7
    lane[...] = second & 127
    line[...] = (
        row_block * (row_block + 1) * 64 + (first & 127) * (row_block + 1) + (second >> 7)
    )

    lanes = iota((128, 128), 0)
    places = iota((GROUP, 128), 0)

    def some_steps(it, carry):
        acc, before = carry
        for k in range(UNROLL):
            t = it * UNROLL + k
            g, b = seq_g[t], seq_b[t]
            spread, where = [], []
            for j in range(2):
                at = pl.ds(2 * b + j, 1)
                spread.append(
                    jnp.where(lanes == lane[at, :], vector[at, :], 0.0).astype(BF)
                )
                where.append(onehot(places == line[at, :] - g * GROUP))
            new = nt(jnp.concatenate(spread, 1), jnp.concatenate(where, 1))
            acc = jnp.where(g == before, acc, 0.0) + new
            tiles[g] = acc
            before = g
        return acc, before

    lax.fori_loop(
        0, total // UNROLL, some_steps, (jnp.zeros((128, GROUP), F32), jnp.int32(-1))
    )

    for g in range(0, GROUPS, 2):
        pair = jnp.concatenate([tiles[g], tiles[g + 1]], axis=1)
        dense[g * GROUP : (g + 2) * GROUP, :] = pair.T

    wide = []
    for big in range(7):
        count = min(128, NAO - big * 128)
        base = 64 * big * (big + 1)
        row = []
        for c in range(big + 1):
            row.append(dense[pl.ds(base + c, count, stride=big + 1), :].astype(BF))
        wide.append(row)
    acc = [None] * 7
    for big in range(7):
        row = wide[big]
        count = row[0].shape[0]
        occ_rows = occ_t[:, big * 128 : big * 128 + count]
        for c in range(big + 1):
            term = nn(occ_rows, row[c])
            acc[c] = term if acc[c] is None else acc[c] + term
    for big in range(7):
        row = wide[big]
        count = row[0].shape[0]
        same = iota((count, 128), 0) == iota((count, 128), 1)
        row = row[:-1] + [jnp.where(same, jnp.zeros((), BF), row[-1])]
        full = row[0] if big == 0 else jnp.concatenate(row, axis=1)
        term = nt(occ_t[:, : (big + 1) * 128], full)
        total_block = acc[big][:, :count] + term
        out[:, big * 128 : big * 128 + count] = total_block[: out.shape[0]]


def half_transform(vector, pairs, occupied):
    vmem = pl.BlockSpec(memory_space=pltpu.VMEM)
    count, nocc = pairs.shape[0], occupied.shape[1]
    blocks = count // BLOCK
    last = pairs.reshape(blocks, BLOCK)[:, -1]
    occ_t = jnp.pad(occupied.T, ((0, 128 - nocc), (0, 896 - NAO)))
    total = -(-(GROUPS + blocks - 1) // UNROLL) * UNROLL
    return pl.pallas_call(
        half_kernel,
        out_shape=jax.ShapeDtypeStruct((nocc, NAO), F32),
        in_specs=[pl.BlockSpec(memory_space=pltpu.SMEM), vmem, vmem, vmem],
        out_specs=vmem,
        scratch_shapes=[
            pltpu.VMEM((count // 128, 128), I32),
            pltpu.VMEM((count // 128, 128), I32),
            pltpu.VMEM((GROUPS + UNROLL, 128, GROUP), F32),
            pltpu.VMEM((GROUPS * GROUP, 128), F32),
            pltpu.SMEM((total,), I32),
            pltpu.SMEM((total,), I32),
        ],
        compiler_params=pltpu.CompilerParams(vmem_limit_bytes=40 * 1024 * 1024),
        name="half",
    )(last, pairs.reshape(count // 128, 128), vector, occ_t)


def per_device(dims, pivots, panel, prior, finished, pairs, occupied):
    plan = Plan(dims, prior.shape[1], prior.shape[0])
    product, vector = communicate(plan, pivots, prior, finished)
    halves = half_transform(vector, pairs, occupied)
    return panel - product, halves[None]


def build(mesh, dims):
    return jax.shard_map(
        functools.partial(per_device, dims),
        mesh=mesh,
        in_specs=(
            P(),
            P(("row", "col"), None),
            P(("row", "col"), None),
            P(("row", "col"), None),
            P(),
            P(),
        ),
        out_specs=(P(("row", "col"), None), P(("row", "col"), None, None)),
        check_vma=False,
    )


def solution(mesh):
    return build(mesh, FULL)
```

time: 255 us -> 55.8 us (0.22)
  blocking collectives: 131 us -> 0 us
  matrix products: 51.2 us -> 0 us
  Pallas kernels: 0 us -> 49.9 us
  local copies, waits for them, and re-layouts: 32.1 us -> 4.31 us
  between operations: 14.2 us -> 0.71 us
  starting transfers between devices: 12.6 us -> 0 us
  other arithmetic: 13.1 us -> 0.67 us
    psum x1 -> x0, blocking collectives: 131 us -> none  [per_device(): pivot_rows = lax.psum(contribution, ('row', 'col')).astype(jnp.bfloat16)]
    dot_general x9 -> x0, matrix products: 51.2 us -> none  [the longest x8 50.6 us: one_block(): jnp.einsum('pi,vpm->vim', coeff_block, spread, preferred_element_type=jnp...]
    pallas_call x0 -> x2, Pallas kernels: none -> 49.9 us  [the longest x1 37.4 us: communicate(): pl.pallas_call(functools.partial(comm_kernel, plan), out_shape=(jax.Shape...]
    gather x3 -> x0, local copies, waits for them, and re-layouts: 25.8 us -> none  [the longest x1 12.1 us: half_transform(): occ_first = jnp.take(occupied, first_ao, axis=0)]
    all_to_all x1 -> x0, starting transfers between devices: 12.6 us -> none  [per_device(): lax.all_to_all(grouped, 'row', split_axis=1, concat_axis=0, tiled=True)]
    select_n x3 -> x0, other arithmetic: 5.93 us -> none  [the longest x1 2.37 us: per_device(): contribution = jnp.where(owned[:, None], picked, jnp.zeros_like(picked))]
    eq x8 -> x0, other arithmetic: 4.76 us -> none  [one_block(): matches = target_block[:, None] == columns[None, :]]
    unnamed x12 -> x14, local copies, waits for them, and re-layouts: 6.15 us -> 3.24 us
  transfers between devices with their start and end apart: 2 -> 0, of which waited for: 0 -> 0; matrix products, arithmetic and copies ran while one was open for 15% -> 0% of each run, Pallas kernels for 0% -> 0%
where the time goes in v1:
time: 55.8 us; the launch traced here: 55.6 us
  Pallas kernels  49.9 us (89%)
  local copies, waits for them, and re-layouts  4.31 us (8%)
  between operations  0.71 us (1%)
  other arithmetic  0.67 us (1%)
    pallas_call x1, Pallas kernels, communicate(): pl.pallas_call(functools.partial(comm_kernel, plan), out_shape=(jax.Shape...  37.4 us
    pallas_call x1, Pallas kernels, half_transform(): pl.pallas_call(half_kernel, out_shape=jax.ShapeDtypeStruct((nocc, NAO), F...  12.5 us
    unnamed x14, local copies, waits for them, and re-layouts  3.24 us

profile of v1, /device:TPU:1, one launch (start us, length us, event | category | flops | bytes accessed | tf_op | source)
XLA Modules:
  0.0 55.6 jit_solution(13553995823821270583)
XLA Ops:
  0.6 0.0 copy-start.1
  0.6 0.8 %copy.13.refs_0_ = s32[256,1]{1,0:T(8,128)S(1)} copy(s32[256,1]{0,1:T(1,128)} %bitcast.7) | data formatting | bytes 2048 | tf_op jit(solution)/shard_map/reshape | solution.py:324
  1.5 0.1 copy-done.1
  1.6 0.0 copy-start.3
  1.6 0.0 copy-start.2
  1.6 0.2 slice_reduce_fusion.last
  1.8 0.4 copy-done.3
  2.2 0.2 copy-done.2
  2.4 0.0 copy-start
  2.4 1.1 %copy-done = bf16[128,3072]{1,0:T(8,128)(2,1)S(1)} copy-done((bf16[128,3072]{1,0:T(8,128)(2,1)S(1)}, bf16[128,3072]{1,0:T(8,128)(2,1)}, u32[]{:S(2)}) %copy-start) | copy-done | bytes 786456
  3.6 0.0 copy-start.5
  3.6 37.4 %exchange.1 = (f32[128,256]{1,0:T(8,128)S(1)}, f32[256,128]{1,0:T(8,128)S(1)}) custom-call(s32[256,1]{1,0:T(8,128)S(1)} %copy.13.refs_0_, s32[1,256]{1,0:T(1,128)S(1)} %bitcast.8, bf16[128,3072]{1,0:T(8,128)(2,1)S(1)} %copy-done, bf16[128,256]{1,0:T(8,128)(2,1)S(1)} %copy-done.2), custom_call_target="tpu_custom_call" | custom-call | tf_op jit(solution)/shard_map/exchange/pallas_call | solution.py:311
  41.0 0.0 copy-start.4
  41.0 0.0 copy-done.5
  41.0 0.7 %sub.3 = f32[128,256]{1,0:T(8,128)} subtract(f32[128,256]{1,0:T(8,128)S(1)} %copy-done.5, f32[128,256]{1,0:T(8,128)S(1)} %get-tuple-element.4) | non-fusion elementwise | flops 32768 | bytes 393216 | tf_op jit(solution)/shard_map/sub | solution.py:442
  41.6 0.3 copy-done.4
  41.9 0.2 copy.14
  42.1 12.5 %half.1 = f32[120,800]{1,0:T(8,128)S(1)} custom-call(s32[128]{0:T(128)S(1)} %slice_reduce_fusion.last, s32[256,128]{1,0:T(8,128)S(1)} %bitcast.6, f32[256,128]{1,0:T(8,128)S(1)} %get-tuple-element.5.vector, bf16[128,896]{1,0:T(8,128)(2,1)S(1)} %pad.4.occ_t), custom_call_target="tpu_custom_call" | custom-call | tf_op jit(solution)/shard_map/half/pallas_call | solution.py:420
  54.6 0.9 %copy.15 = f32[1,120,800]{1,2,0:T(8,128)} copy(f32[1,120,800]{2,1,0:T(8,128)S(1)} %bitcast.5) | data formatting | bytes 768000
  (2 shorter events, 0.1 us)
Async XLA Ops:
  0.6 0.9 %copy-start.1 = (s32[32768]{0:T(1024)S(1)}, s32[32768]{0:T(1024)}, u32[]{:S(2)}) copy-start(s32[32768]{0:T(1024)} %param.10) | copy-start | bytes 393220
  1.6 0.7 %copy-start.3 = (s32[256]{0:T(256)S(1)}, s32[256]{0:T(256)}, u32[]{:S(2)}) copy-start(s32[256]{0:T(256)} %param.6) | copy-start | bytes 3076
  1.6 0.8 %copy-start.2 = (bf16[128,256]{1,0:T(8,128)(2,1)S(1)}, bf16[128,256]{1,0:T(8,128)(2,1)}, u32[]{:S(2)}) copy-start(bf16[128,256]{1,0:T(8,128)(2,1)} %refs_3_.1) | copy-start | bytes 196612
  2.4 1.1 %copy-start = (bf16[128,3072]{1,0:T(8,128)(2,1)S(1)}, bf16[128,3072]{1,0:T(8,128)(2,1)}, u32[]{:S(2)}) copy-start(bf16[128,3072]{1,0:T(8,128)(2,1)} %refs_2_.1) | copy-start | bytes 2359300
  3.6 37.4 %copy-start.5 = (f32[128,256]{1,0:T(8,128)S(1)}, f32[128,256]{1,0:T(8,128)}, u32[]{:S(2)}) copy-start(f32[128,256]{1,0:T(8,128)} %param.7) | copy-start | bytes 393220
  41.0 1.0 %copy-start.4 = (bf16[800,120]{1,0:T(8,128)(2,1)S(1)}, bf16[800,120]{1,0:T(8,128)(2,1)}, u32[]{:S(2)}) copy-start(bf16[800,120]{1,0:T(8,128)(2,1)} %param.11) | copy-start | bytes 576004

commit v2 on v1

v2 whole, which is shorter than its diff:
```python
import functools
from collections import namedtuple

import jax
import jax.numpy as jnp
from jax import lax
from jax.experimental import pallas as pl
from jax.experimental.pallas import tpu as pltpu
from jax.sharding import PartitionSpec as P

MESH = pl.DeviceIdType.MESH
BF, F32, I32 = jnp.bfloat16, jnp.float32, jnp.int32
Dims = namedtuple("Dims", ("x", "y", "zh", "zl", "c"))
FULL = Dims(4, 4, 4, 2, 2)

NAO = 800
GROUP = 64
BLOCK = 256
GROUPS = 46
UNROLL = 8
MASK_UNROLL = 4

UNIT_TILES = (2, 5, 5)
UNIT_ORDERS = (("x", "y", "z"), ("y", "z", "x"), ("z", "x", "y"))


def nt(a, b):
    return lax.dot_general(a, b, (((1,), (1,)), ((), ())), preferred_element_type=F32)


def nn(a, b):
    return lax.dot_general(a, b, (((1,), (0,)), ((), ())), preferred_element_type=F32)


def iota(shape, dim):
    return lax.broadcasted_iota(I32, shape, dim)


def log2(n):
    assert n & (n - 1) == 0
    return n.bit_length() - 1


def mod(v, n):
    return v & (n - 1)


def div(v, n):
    return v >> log2(n)


def onehot(cond):
    return jnp.where(cond, 1.0, 0.0).astype(BF)


def coordinates(dims, device):
    col = mod(device, dims.y * dims.zl)
    row = div(device, dims.y * dims.zl)
    core = mod(row, dims.c)
    x = mod(div(row, dims.c), dims.x)
    zh = div(row, dims.c * dims.x)
    return dict(x=x, y=div(col, dims.zl), z=zh * dims.zl + mod(col, dims.zl), c=core)


def mesh_id(dims, p):
    row = (div(p["z"], dims.zl) * dims.x + p["x"]) * dims.c + p["c"]
    col = p["y"] * dims.zl + mod(p["z"], dims.zl)
    return (row, col)


class Plan:
    def __init__(self, dims, k, rows):
        self.dims = dims
        self.size = dict(x=dims.x, y=dims.y, z=dims.zh * dims.zl, c=dims.c)
        self.n = dims.x * dims.y * dims.zh * dims.zl * dims.c
        self.slots = 2 * self.n
        self.kt_half = k // 128 // 2
        self.rows = rows
        self.units = []
        first = 0
        for tiles, order in zip(UNIT_TILES, UNIT_ORDERS):
            self.units.append(
                dict(
                    tiles=tiles,
                    first=first,
                    order=order,
                    r1=-(-4 * tiles // 8) * 8,
                    n=[self.size[a] for a in order],
                )
            )
            first += tiles
        assert first == self.kt_half
        self.plane = dims.x * dims.y
        self.pole = self.size["z"] * dims.c


def move(me, **changes):
    return {**me, **changes}


def far_first(count):
    return sorted(range(1, count), key=lambda by: (-min(by, count - by), by))


def fused_kernel(plan, *refs):
    dims, size, n = plan.dims, plan.size, plan.n
    nu = len(plan.units)
    (pivots_in, prior_in, finished_in, pairs_in, occupied_in, out, halves) = refs[:7]
    scratch = list(refs[7:])
    take = lambda count: [scratch.pop(0) for _ in range(count)]
    (pivots, prior, finished, pairs, occupied) = take(5)
    first_out = take(nu)
    first_in = take(nu)
    gathered = take(nu)
    (partner_prior, part_out, part_in, a_out, a_in, b_out, b_in) = take(7)
    (lane, line, vector, table, masks, wheres, slots, dense, full, steps_at) = take(10)
    (load, send1, recv1, send2, recv2, send3, recv3, send_a, recv_a, send_b, recv_b,
     send_p, recv_p, send_q, recv_q, table_sem) = take(16)

    own = lax.axis_index("row") * (dims.y * dims.zl) + lax.axis_index("col")
    me = coordinates(dims, own)
    core = me["c"]
    other = move(me, c=1 - core)
    npiv = pivots.shape[1]

    def step(axis, by):
        return mod(me[axis] + by, size[axis])

    lines = []
    for axis in ("x", "y", "z"):
        for by in range(1, size[axis]):
            for c in (core, 1 - core):
                lines.append(move(me, **{axis: step(axis, by), "c": c}))
    plane_peers = []
    for bx in range(dims.x):
        for by in range(dims.y):
            if bx or by:
                far = min(bx, dims.x - bx) + min(by, dims.y - by)
                plane_peers.append((-far, move(me, x=step("x", bx), y=step("y", by))))
    plane_peers = [p for _, p in sorted(plane_peers, key=lambda item: item[0])]
    corners = []
    for bx in range(1, dims.x):
        for by in range(1, dims.y):
            corners.append(move(me, x=step("x", bx), y=step("y", by)))
    pole_peers = []
    for bz in far_first(size["z"]) + [0]:
        for c in (core, 1 - core):
            if bz or c is not core:
                pole_peers.append(move(me, z=step("z", bz), c=c))
    peers = lines + corners + [other]

    barrier = pltpu.get_barrier_semaphore()
    for p in peers:
        pl.semaphore_signal(barrier, inc=1, device_id=mesh_id(dims, p), device_id_type=MESH)

    loads = []
    for i, (src, dst) in enumerate(
        ((pivots_in, pivots), (prior_in, prior), (finished_in, finished),
         (pairs_in, pairs), (occupied_in, occupied))
    ):
        copy = pltpu.make_async_copy(src, dst, load.at[i])
        copy.start()
        loads.append(copy)

    def remote(src, dst, send, recv, p):
        copy = pltpu.make_async_remote_copy(
            src_ref=src, dst_ref=dst, send_sem=send, recv_sem=recv,
            device_id=mesh_id(dims, p), device_id_type=MESH,
        )
        copy.start()

    def wait_bytes(ref, sem):
        pltpu.make_async_copy(ref, ref, sem).wait()

    loads[0].wait()
    piv_row = jnp.broadcast_to(pivots[...], (128, npiv))
    piv_col = piv_row.astype(F32).T.astype(I32)
    here = onehot(piv_col == own * plan.rows + iota((npiv, plan.rows), 1))
    has = nn(jnp.ones((32, npiv), BF), here)
    before = onehot(iota((plan.rows, plan.rows), 0) < iota((plan.rows, plan.rows), 1))
    rank = nn(has.astype(BF), before)
    q = iota((32, plan.rows), 0)
    wanted = (mod(q, 4) - core * 2).astype(F32)
    select = jnp.where((has > 0.5) & (rank == wanted), 1.0, 0.0).astype(BF)
    loads[1].wait()
    for h in range(2):
        for u, unit in enumerate(plan.units):
            k0 = (h * plan.kt_half + unit["first"]) * 128
            rows = nn(select, prior[:, k0 : k0 + unit["tiles"] * 128])
            r1 = unit["r1"]
            part = jnp.zeros((r1, 128), F32)
            which = div(iota((r1, 128), 0), 4)
            for kt in range(unit["tiles"]):
                part = jnp.where(which == kt, rows[:r1, kt * 128 : (kt + 1) * 128], part)
            first_out[u][h] = part.astype(BF)
    for u, unit in enumerate(plan.units):
        first_in[u][me[unit["order"][0]] * dims.c + core] = first_out[u][core]

    loads[2].wait()
    r = iota((n, n), 0)
    v = coordinates(dims, iota((n, n), 1))
    spot = ((v["x"] * dims.y + v["y"]) * size["z"] + v["z"]) * dims.c + v["c"]
    a_rows = nt(onehot(r == spot), finished[...]).astype(BF)
    for i in range(plan.plane):
        a_out[i] = a_rows[i * plan.pole : (i + 1) * plan.pole]
    my_plane = me["x"] * dims.y + me["y"]
    my_pole = me["z"] * dims.c + core
    a_in[my_plane] = a_out[my_plane]

    pl.semaphore_wait(barrier, len(peers))

    for u, unit in enumerate(plan.units):
        axis = unit["order"][0]
        for by in far_first(size[axis]) + [0]:
            for c in (core, 1 - core):
                if by or c is not core:
                    remote(
                        first_out[u].at[c], first_in[u].at[me[axis] * dims.c + core],
                        send1.at[u], recv1.at[u], move(me, **{axis: step(axis, by), "c": c}),
                    )
    for p in plane_peers:
        remote(a_out.at[p["x"] * dims.y + p["y"]], a_in.at[my_plane], send_a, recv_a, p)
    half = plan.kt_half * 128
    remote(
        prior.at[:, pl.ds(pl.multiple_of((1 - core) * half, half), half)],
        partner_prior, send_p, recv_p, other,
    )

    loads[3].wait()
    flat = pairs[...].astype(F32)
    first = jnp.floor((flat + 0.5) * (1.0 / NAO)).astype(I32)
    second = pairs[...] - first * NAO
    row_block = first >> 7
    lane[...] = second & 127
    line[...] = (
        row_block * (row_block + 1) * 64 + (first & 127) * (row_block + 1) + (second >> 7)
    )
    blocks = n // 2
    total = slots.shape[0]
    last = jnp.broadcast_to(line[:, 127:128], (n, 128)) >> log2(GROUP)
    done = (mod(iota((n, 128), 0), 2) == 1) & (last <= iota((n, 128), 1))
    count = jnp.sum(jnp.where(done, 1.0, 0.0), axis=0, keepdims=True)
    leave = jnp.minimum(count, blocks - 1.0) + iota((1, 128), 1).astype(F32)
    leave_col = jnp.broadcast_to(leave, (128, 128)).T
    real = iota((128, 128), 0) < GROUPS
    rows = [leave]
    for t0 in (0, 128):
        past = real & (leave_col < (iota((128, 128), 1) + t0).astype(F32))
        rows.append(jnp.sum(jnp.where(past, 1.0, 0.0), axis=0, keepdims=True))
    which = iota((8, 128), 0)
    packed = jnp.zeros((8, 128), F32)
    for i, row in enumerate(rows):
        packed = jnp.where(which == i, jnp.broadcast_to(row, (8, 128)), packed)
    table[...] = packed.astype(I32)
    copy = pltpu.make_async_copy(table, steps_at, table_sem)
    copy.start()

    lanes = iota((128, 128), 0)
    places = iota((GROUP, 128), 0)

    def make_masks(it, carry):
        for k in range(MASK_UNROLL):
            d = it * MASK_UNROLL + k
            spread = jnp.where(lanes == lane[pl.ds(d, 1), :], 1.0, 0.0)
            masks[d] = spread.T.astype(BF)
        return carry

    def at_step(t):
        g = steps_at[1 + div(t, 128), mod(t, 128)]
        return g, jnp.clip(t - g, 0, blocks - 1)

    def make_wheres(it, carry):
        for k in range(UNROLL):
            t = it * UNROLL + k
            g, b = at_step(t)
            where = [
                onehot(places == line[pl.ds(2 * b + j, 1), :] - g * GROUP) for j in range(2)
            ]
            wheres[t] = jnp.concatenate(where, axis=1)
        return carry

    mask_steps = n // MASK_UNROLL
    lax.fori_loop(0, mask_steps // 2, make_masks, 0)

    def block_of(u, i2):
        n1, n2, n3 = plan.units[u]["n"]
        base = pl.multiple_of((me[plan.units[u]["order"][2]] * n2 + i2) * (n1 * 4), n1 * 4)
        return gathered[u].at[:, pl.ds(base, n1 * 4)]

    def pass_on(u, i2):
        unit = plan.units[u]
        a3 = unit["order"][2]
        block = block_of(u, i2)
        for by in far_first(unit["n"][2]):
            remote(block, block, send3.at[u], recv3.at[u], move(me, **{a3: step(a3, by)}))

    for u, unit in enumerate(plan.units):
        n1, n2, n3 = unit["n"]
        a1, a2, a3 = unit["order"]
        r1, tiles = unit["r1"], unit["tiles"]
        wait_bytes(first_in[u].at[pl.ds(0, n1 * dims.c - 1)], recv1.at[u])
        got = first_in[u][...].reshape(n1 * dims.c * r1, 128)
        shape = (tiles * n1 * 4, n1 * dims.c * r1)
        ro, ci = iota(shape, 0), iota(shape, 1)
        kt, slot = div(ro, n1 * 4), mod(ro, 4)
        target = (mod(div(ro, 4), n1) * dims.c + div(slot, 2)) * r1 + kt * 4 + slot
        rows = nn(onehot(ci == target), got).astype(BF)
        base = pl.multiple_of((me[a3] * n2 + me[a2]) * (n1 * 4), n1 * 4)
        for t in range(tiles):
            gathered[u][t, pl.ds(base, n1 * 4)] = rows[t * n1 * 4 : (t + 1) * n1 * 4]
        block = block_of(u, me[a2])
        for by in far_first(n2):
            remote(
                block, block, send2.at[u], recv2.at[u, me[a2]], move(me, **{a2: step(a2, by)})
            )
        pass_on(u, me[a2])

    wait_bytes(a_in.at[pl.ds(0, plan.plane - 1)], recv_a)
    mixed = a_in[...].reshape(n, plan.rows)
    source = mod(r, plan.plane) * plan.pole + div(r, plan.plane)
    b_rows = nn(onehot(iota((n, n), 1) == source), mixed).astype(BF)
    for i in range(plan.pole):
        b_out[i] = b_rows[i * plan.plane : (i + 1) * plan.plane]
    b_in[my_pole] = b_out[my_pole]
    for p in pole_peers:
        remote(b_out.at[p["z"] * dims.c + p["c"]], b_in.at[my_pole], send_b, recv_b, p)

    copy.wait()
    lax.fori_loop(0, total // UNROLL, make_wheres, 0)

    for u, unit in enumerate(plan.units):
        a2 = unit["order"][1]
        for by in reversed(far_first(unit["n"][1])):
            i2 = step(a2, by)
            wait_bytes(block_of(u, i2), recv2.at[u, i2])
            pass_on(u, i2)

    lax.fori_loop(mask_steps // 2, mask_steps, make_masks, 0)

    wait_bytes(b_in.at[pl.ds(0, plan.pole - 1)], recv_b)
    mixed = b_in[...].reshape(n, plan.rows)
    w = coordinates(dims, r)
    source = (w["z"] * dims.c + w["c"]) * plan.plane + w["x"] * dims.y + w["y"]
    vector[...] = nn(onehot(iota((n, n), 1) == source), mixed)

    def scatter(it, carry):
        acc, before = carry
        for k in range(UNROLL):
            t = it * UNROLL + k
            g, b = at_step(t)
            scale = [
                jnp.broadcast_to(vector[pl.ds(2 * b + j, 1), :], (GROUP, 128)).astype(BF)
                for j in range(2)
            ]
            left = wheres[t] * jnp.concatenate(scale, axis=1)
            right = masks[pl.ds(2 * b, 2)].reshape(BLOCK, 128)
            acc = jnp.where(g == before, acc, 0.0) + nn(left, right)
            slots[t] = acc
            before = g
        return acc, before

    lax.fori_loop(
        0, total // UNROLL, scatter, (jnp.zeros((GROUP, 128), F32), jnp.int32(-1))
    )
    for g in range(GROUPS):
        dense[g * GROUP : (g + 1) * GROUP, :] = slots[jnp.clip(steps_at[0, g], 0, total - 1)]

    same = iota((128, 128), 0) == iota((128, 128), 1)
    for big in range(7):
        height = min(128, NAO - big * 128)
        base = 64 * big * (big + 1)
        for c in range(big + 1):
            tile = dense[pl.ds(base + c, height, stride=big + 1), :]
            if height < 128:
                tile = jnp.concatenate([tile, jnp.zeros((128 - height, 128), F32)], axis=0)
            flip = tile.T
            if c == big:
                tile = jnp.where(same, tile, tile + flip)
            else:
                full[c * 128 : (c + 1) * 128, big * 128 : (big + 1) * 128] = flip.astype(BF)
            full[big * 128 : (big + 1) * 128, c * 128 : (c + 1) * 128] = tile.astype(BF)
    loads[4].wait()
    for big in range(7):
        height = min(128, NAO - big * 128)
        rows = nn(full[big * 128 : (big + 1) * 128, :NAO], occupied[...])
        halves[big * 128 : big * 128 + height, :] = rows[:height]

    lower = []
    for j0 in range(0, npiv, 128):
        pr = piv_row[:1, j0 : j0 + 128] if npiv >= 128 else piv_row[:1]
        pc = piv_col[:, : pr.shape[1]]
        lower.append(onehot((div(pc, plan.rows) == div(pr, plan.rows)) & (pr < pc)))
    lower = jnp.concatenate(lower, axis=1)
    place = nn(lower, jnp.ones((npiv, 128), BF)).astype(I32)
    o = coordinates(dims, div(piv_col, plan.rows))

    wait_bytes(partner_prior, recv_p)
    mine = jnp.zeros((plan.rows, npiv), F32)
    theirs = jnp.zeros((plan.rows, npiv), F32)
    for u, unit in enumerate(plan.units):
        n1, n2, n3 = unit["n"]
        a1, a2, a3 = unit["order"]
        tiles = unit["tiles"]
        wait_bytes(gathered[u].at[:, pl.ds(0, n2 * n1 * 4 * (n3 - 1))], recv3.at[u])
        at = ((o[a3] * n2 + o[a2]) * n1 + o[a1]) * 4 + o["c"] * 2 + place
        pick = jnp.concatenate(
            [onehot(iota((npiv, 128), 1) + s == at) for s in range(0, plan.slots, 128)], axis=1
        )
        pick = pick[:, : plan.slots]
        rows = jnp.concatenate(
            [nn(pick, gathered[u][t]).astype(BF) for t in range(tiles)], axis=1
        )
        k0 = unit["first"] * 128
        at_k = pl.multiple_of(core * half + k0, 128)
        mine += nt(prior[:, pl.ds(at_k, tiles * 128)], rows)
        theirs += nt(partner_prior[:, k0 : k0 + tiles * 128], rows)
    part_out[...] = theirs
    remote(part_out, part_in, send_q, recv_q, other)

    for u, unit in enumerate(plan.units):
        n1, n2, n3 = unit["n"]
        wait_bytes(first_in[u].at[pl.ds(0, n1 * dims.c - 1)], send1.at[u])
        wait_bytes(gathered[u].at[:, pl.ds(0, n1 * 4 * (n2 - 1))], send2.at[u])
        wait_bytes(gathered[u].at[:, pl.ds(0, n2 * n1 * 4 * (n3 - 1))], send3.at[u])
    wait_bytes(a_in.at[pl.ds(0, plan.plane - 1)], send_a)
    wait_bytes(b_in.at[pl.ds(0, plan.pole - 1)], send_b)
    wait_bytes(partner_prior, send_p)
    wait_bytes(part_in, recv_q)
    wait_bytes(part_out, send_q)
    out[...] = mine + part_in[...]


def run_kernel(plan, pivots, prior, finished, pairs, occupied):
    npiv = pivots.shape[0]
    vmem = pl.BlockSpec(memory_space=pltpu.VMEM)
    anywhere = pl.BlockSpec(memory_space=pl.ANY)
    dma = pltpu.SemaphoreType.DMA
    nu = len(plan.units)
    n, rows = plan.n, plan.rows
    blocks = n // 2
    total = -(-(GROUPS + blocks - 1) // UNROLL) * UNROLL
    scratch = [
        pltpu.VMEM((1, npiv), I32),
        pltpu.VMEM(prior.shape, BF),
        pltpu.VMEM(finished.shape, BF),
        pltpu.VMEM((n, rows), I32),
        pltpu.VMEM(occupied.shape, BF),
    ]
    scratch += [pltpu.VMEM((2, u["r1"], 128), BF) for u in plan.units]
    scratch += [pltpu.VMEM((u["n"][0] * plan.dims.c, u["r1"], 128), BF) for u in plan.units]
    scratch += [pltpu.VMEM((u["tiles"], plan.slots, 128), BF) for u in plan.units]
    scratch += [
        pltpu.VMEM((rows, plan.kt_half * 128), BF),
        pltpu.VMEM((rows, npiv), F32),
        pltpu.VMEM((rows, npiv), F32),
        pltpu.VMEM((plan.plane, plan.pole, rows), BF),
        pltpu.VMEM((plan.plane, plan.pole, rows), BF),
        pltpu.VMEM((plan.pole, plan.plane, rows), BF),
        pltpu.VMEM((plan.pole, plan.plane, rows), BF),
        pltpu.VMEM((n, 128), I32),
        pltpu.VMEM((n, 128), I32),
        pltpu.VMEM((n, 128), F32),
        pltpu.VMEM((8, 128), I32),
        pltpu.VMEM((n, 128, 128), BF),
        pltpu.VMEM((total, GROUP, BLOCK), BF),
        pltpu.VMEM((total, GROUP, 128), F32),
        pltpu.VMEM((GROUPS * GROUP, 128), F32),
        pltpu.VMEM((896, 896), BF),
        pltpu.SMEM((8, 128), I32),
    ]
    scratch += [dma((5,)), dma((nu,)), dma((nu,)), dma((nu,)), dma((nu, 8))]
    scratch += [dma((nu,)), dma((nu,))] + [dma] * 9
    return pl.pallas_call(
        functools.partial(fused_kernel, plan),
        out_shape=(
            jax.ShapeDtypeStruct((rows, npiv), F32),
            jax.ShapeDtypeStruct((NAO, occupied.shape[1]), F32),
        ),
        in_specs=[anywhere] * 5,
        out_specs=(vmem, vmem),
        scratch_shapes=scratch,
        compiler_params=pltpu.CompilerParams(
            collective_id=0, has_side_effects=True, vmem_limit_bytes=34 * 1024 * 1024
        ),
        name="fused",
    )(pivots.reshape(1, npiv), prior, finished, pairs.reshape(n, rows), occupied)


def per_device(dims, pivots, panel, prior, finished, pairs, occupied):
    plan = Plan(dims, prior.shape[1], prior.shape[0])
    product, flipped = run_kernel(plan, pivots, prior, finished, pairs, occupied)
    return panel - product, flipped.T[None]


def build(mesh, dims):
    return jax.shard_map(
        functools.partial(per_device, dims),
        mesh=mesh,
        in_specs=(
            P(),
            P(("row", "col"), None),
            P(("row", "col"), None),
            P(("row", "col"), None),
            P(),
            P(),
        ),
        out_specs=(P(("row", "col"), None), P(("row", "col"), None, None)),
        check_vma=False,
    )


def solution(mesh):
    return build(mesh, FULL)
```

time: 55.8 us -> 43.6 us (0.78)
  Pallas kernels: 49.9 us -> 36.8 us
  local copies, waits for them, and re-layouts: 4.31 us -> 5.23 us
    pallas_call x2 -> x1, Pallas kernels: 49.9 us -> 36.8 us  [run_kernel(): pl.pallas_call(functools.partial(fused_kernel, plan), out_shape=(jax.Shap...]
    unnamed x14 -> x13, local copies, waits for them, and re-layouts: 3.24 us -> 5.23 us
    reshape x2 -> x0, local copies, waits for them, and re-layouts: 0.88 us -> none  [the longest x1 0.84 us: communicate(): pivots.reshape(npiv, 1)]
where the time goes in v2:
time: 43.6 us; the launch traced here: 43.3 us
  Pallas kernels  36.8 us (84%)
  local copies, waits for them, and re-layouts  5.23 us (12%)
  other arithmetic  0.67 us (2%)
  between operations  0.66 us (2%)
    pallas_call x1, Pallas kernels, run_kernel(): pl.pallas_call(functools.partial(fused_kernel, plan), out_shape=(jax.Shap...  36.8 us
    unnamed x13, local copies, waits for them, and re-layouts  5.23 us

profile of v2, /device:TPU:1, one launch (start us, length us, event | category | flops | bytes accessed | tf_op | source)
XLA Modules:
  0.0 43.3 jit_solution(8388495133538051104)
XLA Ops:
  0.6 0.0 copy-start.4
  0.6 0.7 %copy-done.4 = s32[256]{0:T(256)S(1)} copy-done((s32[256]{0:T(256)S(1)}, s32[256]{0:T(256)}, u32[]{:S(2)}) %copy-start.4) | copy-done | bytes 1048
  1.3 0.0 copy-start
  1.3 1.1 %copy-done = bf16[128,3072]{1,0:T(8,128)(2,1)S(1)} copy-done((bf16[128,3072]{1,0:T(8,128)(2,1)S(1)}, bf16[128,3072]{1,0:T(8,128)(2,1)}, u32[]{:S(2)}) %copy-start) | copy-done | bytes 786456
  2.4 0.0 copy-start.1
  2.4 0.9 %copy-done.1 = bf16[800,120]{1,0:T(8,128)(2,1)S(1)} copy-done((bf16[800,120]{1,0:T(8,128)(2,1)S(1)}, bf16[800,120]{1,0:T(8,128)(2,1)}, u32[]{:S(2)}) %copy-start.1) | copy-done | bytes 192024
  3.4 0.0 copy-start.2
  3.4 0.9 %copy-done.2 = s32[32768]{0:T(1024)S(1)} copy-done((s32[32768]{0:T(1024)S(1)}, s32[32768]{0:T(1024)}, u32[]{:S(2)}) %copy-start.2) | copy-done | bytes 131096
  4.3 0.0 copy-start.3
  4.3 0.8 %copy-done.3 = bf16[128,256]{1,0:T(8,128)(2,1)S(1)} copy-done((bf16[128,256]{1,0:T(8,128)(2,1)S(1)}, bf16[128,256]{1,0:T(8,128)(2,1)}, u32[]{:S(2)}) %copy-start.3) | copy-done | bytes 65560
  5.1 0.0 copy-start.5
  5.1 36.8 %fused.1 = (f32[128,256]{1,0:T(8,128)S(1)}, f32[800,120]{1,0:T(8,128)S(1)}) custom-call(s32[1,256]{1,0:T(1,128)S(1)} %bitcast.7, bf16[128,3072]{1,0:T(8,128)(2,1)S(1)} %copy-done, bf16[128,256]{1,0:T(8,128)(2,1)S(1)} %copy-done.3, s32[256,128]{1,0:T(8,128)S(1)} %bitcast.6, bf16[800,120]{1,0:T(8,128)(2,1)S(1)} %copy-done.1), custom_call_target="tpu_custom_call" | custom-call | tf_op jit(solution)/shard_map/fused/pallas_call | solution.py:473
  41.9 0.0 copy-done.5
  41.9 0.7 %sub.3 = f32[128,256]{1,0:T(8,128)} subtract(f32[128,256]{1,0:T(8,128)S(1)} %copy-done.5, f32[128,256]{1,0:T(8,128)S(1)} %get-tuple-element.4) | non-fusion elementwise | flops 32768 | bytes 393216 | tf_op jit(solution)/shard_map/sub | solution.py:492
  42.6 0.8 %copy.9 = f32[1,120,800]{1,2,0:T(8,128)} copy(f32[1,120,800]{1,2,0:T(8,128)S(1)} %bitcast.5) | data formatting | bytes 768000
Async XLA Ops:
  0.6 0.7 %copy-start.4 = (s32[256]{0:T(256)S(1)}, s32[256]{0:T(256)}, u32[]{:S(2)}) copy-start(s32[256]{0:T(256)} %param.6) | copy-start | bytes 3076
  1.3 1.1 %copy-start = (bf16[128,3072]{1,0:T(8,128)(2,1)S(1)}, bf16[128,3072]{1,0:T(8,128)(2,1)}, u32[]{:S(2)}) copy-start(bf16[128,3072]{1,0:T(8,128)(2,1)} %refs_1_.1) | copy-start | bytes 2359300
  2.4 0.9 %copy-start.1 = (bf16[800,120]{1,0:T(8,128)(2,1)S(1)}, bf16[800,120]{1,0:T(8,128)(2,1)}, u32[]{:S(2)}) copy-start(bf16[800,120]{1,0:T(8,128)(2,1)} %refs_4_.1) | copy-start | bytes 576004
  3.4 0.9 %copy-start.2 = (s32[32768]{0:T(1024)S(1)}, s32[32768]{0:T(1024)}, u32[]{:S(2)}) copy-start(s32[32768]{0:T(1024)} %param.10) | copy-start | bytes 393220
  4.3 0.8 %copy-start.3 = (bf16[128,256]{1,0:T(8,128)(2,1)S(1)}, bf16[128,256]{1,0:T(8,128)(2,1)}, u32[]{:S(2)}) copy-start(bf16[128,256]{1,0:T(8,128)(2,1)} %refs_2_.1) | copy-start | bytes 196612
  5.1 36.8 %copy-start.5 = (f32[128,256]{1,0:T(8,128)S(1)}, f32[128,256]{1,0:T(8,128)}, u32[]{:S(2)}) copy-start(f32[128,256]{1,0:T(8,128)} %param.7) | copy-start | bytes 393220

commit v3 on v2

--- a/solution.py
+++ b/solution.py
@@ -1,4 +1,5 @@
 import functools
+import math
 from collections import namedtuple
 
 import jax
@@ -17,8 +18,9 @@
 GROUP = 64
 BLOCK = 256
 GROUPS = 46
-UNROLL = 8
-MASK_UNROLL = 4
+UNROLL = 22
+WHERE_UNROLL = 8
+MASK_UNROLL = 16
 
 UNIT_TILES = (2, 5, 5)
 UNIT_ORDERS = (("x", "y", "z"), ("y", "z", "x"), ("z", "x", "y"))
@@ -98,6 +100,11 @@
     return {**me, **changes}
 
 
+def steps_of(blocks):
+    both = UNROLL * WHERE_UNROLL // math.gcd(UNROLL, WHERE_UNROLL)
+    return -(-(GROUPS + blocks - 1) // both) * both
+
+
 def far_first(count):
     return sorted(range(1, count), key=lambda by: (-min(by, count - by), by))
 
@@ -113,7 +120,7 @@
     first_in = take(nu)
     gathered = take(nu)
     (partner_prior, part_out, part_in, a_out, a_in, b_out, b_in) = take(7)
-    (lane, line, vector, table, masks, wheres, slots, dense, full, steps_at) = take(10)
+    (lane, line, vector, table, masks, wheres, slots, dense, full, picks, steps_at) = take(11)
     (load, send1, recv1, send2, recv2, send3, recv3, send_a, recv_a, send_b, recv_b,
      send_p, recv_p, send_q, recv_q, table_sem) = take(16)
 
@@ -261,8 +268,7 @@
     def make_masks(it, carry):
         for k in range(MASK_UNROLL):
             d = it * MASK_UNROLL + k
-            spread = jnp.where(lanes == lane[pl.ds(d, 1), :], 1.0, 0.0)
-            masks[d] = spread.T.astype(BF)
+            masks[d] = onehot(lanes == lane[pl.ds(d, 1), :]).T
         return carry
 
     def at_step(t):
@@ -270,8 +276,8 @@
         return g, jnp.clip(t - g, 0, blocks - 1)
 
     def make_wheres(it, carry):
-        for k in range(UNROLL):
-            t = it * UNROLL + k
+        for k in range(WHERE_UNROLL):
+            t = it * WHERE_UNROLL + k
             g, b = at_step(t)
             where = [
                 onehot(places == line[pl.ds(2 * b + j, 1), :] - g * GROUP) for j in range(2)
@@ -279,7 +285,7 @@
             wheres[t] = jnp.concatenate(where, axis=1)
         return carry
 
-    mask_steps = n // MASK_UNROLL
+    mask_steps = max(1, n // MASK_UNROLL)
     lax.fori_loop(0, mask_steps // 2, make_masks, 0)
 
     def block_of(u, i2):
@@ -326,16 +332,37 @@
         remote(b_out.at[p["z"] * dims.c + p["c"]], b_in.at[my_pole], send_b, recv_b, p)
 
     copy.wait()
-    lax.fori_loop(0, total // UNROLL, make_wheres, 0)
-
-    for u, unit in enumerate(plan.units):
+    lax.fori_loop(0, total // WHERE_UNROLL, make_wheres, 0)
+
+    def pass_on_arrivals(u):
+        unit = plan.units[u]
         a2 = unit["order"][1]
         for by in reversed(far_first(unit["n"][1])):
             i2 = step(a2, by)
             wait_bytes(block_of(u, i2), recv2.at[u, i2])
             pass_on(u, i2)
 
+    pass_on_arrivals(0)
+    pass_on_arrivals(2)
     lax.fori_loop(mask_steps // 2, mask_steps, make_masks, 0)
+
+    lower = []
+    for j0 in range(0, npiv, 128):
+        pr = piv_row[:1, j0 : j0 + 128] if npiv >= 128 else piv_row[:1]
+        pc = piv_col[:, : pr.shape[1]]
+        lower.append(onehot((div(pc, plan.rows) == div(pr, plan.rows)) & (pr < pc)))
+    lower = jnp.concatenate(lower, axis=1)
+    place = nn(lower, jnp.ones((npiv, 128), BF)).astype(I32)
+    o = coordinates(dims, div(piv_col, plan.rows))
+    for u, unit in enumerate(plan.units):
+        n1, n2, n3 = unit["n"]
+        a1, a2, a3 = unit["order"]
+        at = ((o[a3] * n2 + o[a2]) * n1 + o[a1]) * 4 + o["c"] * 2 + place
+        pick = jnp.concatenate(
+            [onehot(iota((npiv, 128), 1) + s == at) for s in range(0, plan.slots, 128)], axis=1
+        )
+        picks[u] = pick[:, : plan.slots]
+    pass_on_arrivals(1)
 
     wait_bytes(b_in.at[pl.ds(0, plan.pole - 1)], recv_b)
     mixed = b_in[...].reshape(n, plan.rows)
@@ -385,37 +412,26 @@
         rows = nn(full[big * 128 : (big + 1) * 128, :NAO], occupied[...])
         halves[big * 128 : big * 128 + height, :] = rows[:height]
 
-    lower = []
-    for j0 in range(0, npiv, 128):
-        pr = piv_row[:1, j0 : j0 + 128] if npiv >= 128 else piv_row[:1]
-        pc = piv_col[:, : pr.shape[1]]
-        lower.append(onehot((div(pc, plan.rows) == div(pr, plan.rows)) & (pr < pc)))
-    lower = jnp.concatenate(lower, axis=1)
-    place = nn(lower, jnp.ones((npiv, 128), BF)).astype(I32)
-    o = coordinates(dims, div(piv_col, plan.rows))
-
     wait_bytes(partner_prior, recv_p)
-    mine = jnp.zeros((plan.rows, npiv), F32)
     theirs = jnp.zeros((plan.rows, npiv), F32)
-    for u, unit in enumerate(plan.units):
+    chosen = []
+    for u in (0, 2, 1):
+        unit = plan.units[u]
         n1, n2, n3 = unit["n"]
-        a1, a2, a3 = unit["order"]
         tiles = unit["tiles"]
         wait_bytes(gathered[u].at[:, pl.ds(0, n2 * n1 * 4 * (n3 - 1))], recv3.at[u])
-        at = ((o[a3] * n2 + o[a2]) * n1 + o[a1]) * 4 + o["c"] * 2 + place
-        pick = jnp.concatenate(
-            [onehot(iota((npiv, 128), 1) + s == at) for s in range(0, plan.slots, 128)], axis=1
+        rows = jnp.concatenate(
+            [nn(picks[u], gathered[u][t]).astype(BF) for t in range(tiles)], axis=1
         )
-        pick = pick[:, : plan.slots]
-        rows = jnp.concatenate(
-            [nn(pick, gathered[u][t]).astype(BF) for t in range(tiles)], axis=1
-        )
+        chosen.append((unit, rows))
         k0 = unit["first"] * 128
-        at_k = pl.multiple_of(core * half + k0, 128)
-        mine += nt(prior[:, pl.ds(at_k, tiles * 128)], rows)
         theirs += nt(partner_prior[:, k0 : k0 + tiles * 128], rows)
     part_out[...] = theirs
     remote(part_out, part_in, send_q, recv_q, other)
+    mine = jnp.zeros((plan.rows, npiv), F32)
+    for unit, rows in chosen:
+        at_k = pl.multiple_of(core * half + unit["first"] * 128, 128)
+        mine += nt(prior[:, pl.ds(at_k, unit["tiles"] * 128)], rows)
 
     for u, unit in enumerate(plan.units):
         n1, n2, n3 = unit["n"]
@@ -438,7 +454,7 @@
     nu = len(plan.units)
     n, rows = plan.n, plan.rows
     blocks = n // 2
-    total = -(-(GROUPS + blocks - 1) // UNROLL) * UNROLL
+    total = steps_of(blocks)
     scratch = [
         pltpu.VMEM((1, npiv), I32),
         pltpu.VMEM(prior.shape, BF),
@@ -466,6 +482,7 @@
         pltpu.VMEM((total, GROUP, 128), F32),
         pltpu.VMEM((GROUPS * GROUP, 128), F32),
         pltpu.VMEM((896, 896), BF),
+        pltpu.VMEM((nu, npiv, plan.slots), BF),
         pltpu.SMEM((8, 128), I32),
     ]
     scratch += [dma((5,)), dma((nu,)), dma((nu,)), dma((nu,)), dma((nu, 8))]
@@ -473,23 +490,48 @@
     return pl.pallas_call(
         functools.partial(fused_kernel, plan),
         out_shape=(
-            jax.ShapeDtypeStruct((rows, npiv), F32),
-            jax.ShapeDtypeStruct((NAO, occupied.shape[1]), F32),
+            pltpu.VMEM((rows, npiv), F32),
+            pltpu.VMEM((NAO, occupied.shape[1]), F32),
         ),
         in_specs=[anywhere] * 5,
         out_specs=(vmem, vmem),
         scratch_shapes=scratch,
         compiler_params=pltpu.CompilerParams(
-            collective_id=0, has_side_effects=True, vmem_limit_bytes=34 * 1024 * 1024
+            collective_id=0, has_side_effects=True, vmem_limit_bytes=56 * 1024 * 1024
         ),
         name="fused",
     )(pivots.reshape(1, npiv), prior, finished, pairs.reshape(n, rows), occupied)
 
 
+def finish_kernel(panel, product, flipped, updated, halves, result, sems):
+    first = pltpu.make_async_copy(flipped, halves, sems.at[0])
+    first.start()
+    result[...] = panel[...] - product[...]
+    second = pltpu.make_async_copy(result, updated, sems.at[1])
+    second.start()
+    first.wait()
+    second.wait()
+
+
+def finish(panel, product, flipped):
+    vmem = pl.BlockSpec(memory_space=pltpu.VMEM)
+    hbm = pl.BlockSpec(memory_space=pltpu.HBM)
+    return pl.pallas_call(
+        finish_kernel,
+        out_shape=(pltpu.HBM(panel.shape, F32), pltpu.HBM(flipped.shape, F32)),
+        in_specs=[vmem] * 3,
+        out_specs=(hbm, hbm),
+        scratch_shapes=[pltpu.VMEM(panel.shape, F32), pltpu.SemaphoreType.DMA((2,))],
+        compiler_params=pltpu.CompilerParams(vmem_limit_bytes=4 * 1024 * 1024),
+        name="finish",
+    )(panel, product, flipped)
+
+
 def per_device(dims, pivots, panel, prior, finished, pairs, occupied):
     plan = Plan(dims, prior.shape[1], prior.shape[0])
     product, flipped = run_kernel(plan, pivots, prior, finished, pairs, occupied)
-    return panel - product, flipped.T[None]
+    updated, flipped = finish(panel, product, flipped)
+    return updated, flipped.T[None]
 
 
 def build(mesh, dims):

time: 43.6 us -> 34.6 us (0.79)
  local copies, waits for them, and re-layouts: 5.23 us -> 0.01 us
  Pallas kernels: 36.8 us -> 33.9 us
  other arithmetic: 0.67 us -> 0 us
    unnamed x13 -> x2, local copies, waits for them, and re-layouts: 5.23 us -> 0.01 us
    pallas_call x1 -> x2, Pallas kernels: 36.8 us -> 33.9 us  [the longest x1 33.1 us: run_kernel(): pl.pallas_call(functools.partial(fused_kernel, plan), out_shape=(pltpu.VM...]
    sub x1 -> x0, other arithmetic: 0.67 us -> none  [per_device(): return (panel - product, flipped.T[None])]
where the time goes in v3:
time: 34.6 us; the launch traced here: 34.5 us
  Pallas kernels  33.9 us (98%)
  between operations  0.66 us (2%)
    pallas_call x1, Pallas kernels, run_kernel(): pl.pallas_call(functools.partial(fused_kernel, plan), out_shape=(pltpu.VM...  33.1 us
    pallas_call x1, Pallas kernels, finish(): pl.pallas_call(finish_kernel, out_shape=(pltpu.HBM(panel.shape, F32), plt...  0.81 us

profile of v3, /device:TPU:1, one launch (start us, length us, event | category | flops | bytes accessed | tf_op | source)
XLA Modules:
  0.0 34.5 jit_solution(11852526776812586288)
XLA Ops:
  0.6 0.0 copy-start
  0.6 33.1 %fused.1 = (f32[128,256]{1,0:T(8,128)S(1)}, f32[800,120]{1,0:T(8,128)S(1)}) custom-call(s32[1,256]{1,0:T(1,128)} %bitcast.6, bf16[128,3072]{1,0:T(8,128)(2,1)} %refs_1_.1, bf16[128,256]{1,0:T(8,128)(2,1)} %refs_2_.1, s32[256,128]{1,0:T(8,128)} %bitcast.5, bf16[800,120]{1,0:T(8,128)(2,1)} %refs_4_.1), custom_call_target="tpu_custom_call" | custom-call | tf_op jit(solution)/shard_map/fused/pallas_call | solution.py:490
  33.7 0.0 copy-done
  33.7 0.8 %finish.1 = (f32[128,256]{1,0:T(8,128)}, f32[800,120]{1,0:T(8,128)}) custom-call(f32[128,256]{1,0:T(8,128)S(1)} %copy-done, f32[128,256]{1,0:T(8,128)S(1)} %get-tuple-element.6.product, f32[800,120]{1,0:T(8,128)S(1)} %get-tuple-element.7.flipped), custom_call_target="tpu_custom_call" | custom-call | tf_op jit(solution)/shard_map/finish/pallas_call | solution.py:519
Async XLA Ops:
  0.6 33.1 %copy-start = (f32[128,256]{1,0:T(8,128)S(1)}, f32[128,256]{1,0:T(8,128)}, u32[]{:S(2)}) copy-start(f32[128,256]{1,0:T(8,128)} %panel.1) | copy-start | bytes 393220

commit v4 on v3

--- a/solution.py
+++ b/solution.py
@@ -22,7 +22,7 @@
 WHERE_UNROLL = 8
 MASK_UNROLL = 16
 
-UNIT_TILES = (2, 5, 5)
+UNIT_TILES = (2, 4, 6)
 UNIT_ORDERS = (("x", "y", "z"), ("y", "z", "x"), ("z", "x", "y"))
 
 

time: 34.6 us -> 33.7 us (0.974)
  Pallas kernels: 33.9 us -> 32.9 us
    pallas_call x1, Pallas kernels: 33.1 us -> 32.1 us  [run_kernel(): pl.pallas_call(functools.partial(fused_kernel, plan), out_shape=(pltpu.VM...]
where the time goes in v4:
time: 33.7 us; the launch traced here: 33.6 us
  Pallas kernels  32.9 us (98%)
  between operations  0.66 us (2%)
    pallas_call x1, Pallas kernels, run_kernel(): pl.pallas_call(functools.partial(fused_kernel, plan), out_shape=(pltpu.VM...  32.1 us
    pallas_call x1, Pallas kernels, finish(): pl.pallas_call(finish_kernel, out_shape=(pltpu.HBM(panel.shape, F32), plt...  0.81 us

profile of v4, /device:TPU:1, one launch (start us, length us, event | category | flops | bytes accessed | tf_op | source)
XLA Modules:
  0.0 33.6 jit_solution(16484393780322678164)
XLA Ops:
  0.6 0.0 copy-start
  0.6 32.1 %fused.1 = (f32[128,256]{1,0:T(8,128)S(1)}, f32[800,120]{1,0:T(8,128)S(1)}) custom-call(s32[1,256]{1,0:T(1,128)} %bitcast.6, bf16[128,3072]{1,0:T(8,128)(2,1)} %refs_1_.1, bf16[128,256]{1,0:T(8,128)(2,1)} %refs_2_.1, s32[256,128]{1,0:T(8,128)} %bitcast.5, bf16[800,120]{1,0:T(8,128)(2,1)} %refs_4_.1), custom_call_target="tpu_custom_call" | custom-call | tf_op jit(solution)/shard_map/fused/pallas_call | solution.py:490
  32.8 0.0 copy-done
  32.8 0.8 %finish.1 = (f32[128,256]{1,0:T(8,128)}, f32[800,120]{1,0:T(8,128)}) custom-call(f32[128,256]{1,0:T(8,128)S(1)} %copy-done, f32[128,256]{1,0:T(8,128)S(1)} %get-tuple-element.6.product, f32[800,120]{1,0:T(8,128)S(1)} %get-tuple-element.7.flipped), custom_call_target="tpu_custom_call" | custom-call | tf_op jit(solution)/shard_map/finish/pallas_call | solution.py:519
Async XLA Ops:
  0.6 32.1 %copy-start = (f32[128,256]{1,0:T(8,128)S(1)}, f32[128,256]{1,0:T(8,128)}, u32[]{:S(2)}) copy-start(f32[128,256]{1,0:T(8,128)} %panel.1) | copy-start | bytes 393220

commit v5 on v3

--- a/solution.py
+++ b/solution.py
@@ -300,7 +300,8 @@
         for by in far_first(unit["n"][2]):
             remote(block, block, send3.at[u], recv3.at[u], move(me, **{a3: step(a3, by)}))
 
-    for u, unit in enumerate(plan.units):
+    def begin_second(u):
+        unit = plan.units[u]
         n1, n2, n3 = unit["n"]
         a1, a2, a3 = unit["order"]
         r1, tiles = unit["r1"], unit["tiles"]
@@ -321,6 +322,12 @@
             )
         pass_on(u, me[a2])
 
+    begin_second(1)
+    begin_second(0)
+    copy.wait()
+    lax.fori_loop(0, total // WHERE_UNROLL, make_wheres, 0)
+    begin_second(2)
+
     wait_bytes(a_in.at[pl.ds(0, plan.plane - 1)], recv_a)
     mixed = a_in[...].reshape(n, plan.rows)
     source = mod(r, plan.plane) * plan.pole + div(r, plan.plane)
@@ -331,20 +338,19 @@
     for p in pole_peers:
         remote(b_out.at[p["z"] * dims.c + p["c"]], b_in.at[my_pole], send_b, recv_b, p)
 
-    copy.wait()
-    lax.fori_loop(0, total // WHERE_UNROLL, make_wheres, 0)
-
-    def pass_on_arrivals(u):
+    def pass_on_arrivals(u, first, last):
         unit = plan.units[u]
         a2 = unit["order"][1]
-        for by in reversed(far_first(unit["n"][1])):
+        for by in list(reversed(far_first(unit["n"][1])))[first:last]:
             i2 = step(a2, by)
             wait_bytes(block_of(u, i2), recv2.at[u, i2])
             pass_on(u, i2)
 
-    pass_on_arrivals(0)
-    pass_on_arrivals(2)
+    pass_on_arrivals(0, 0, 8)
+    pass_on_arrivals(1, 0, 4)
     lax.fori_loop(mask_steps // 2, mask_steps, make_masks, 0)
+    pass_on_arrivals(2, 0, 8)
+    pass_on_arrivals(1, 4, 8)
 
     lower = []
     for j0 in range(0, npiv, 128):
@@ -362,8 +368,6 @@
             [onehot(iota((npiv, 128), 1) + s == at) for s in range(0, plan.slots, 128)], axis=1
         )
         picks[u] = pick[:, : plan.slots]
-    pass_on_arrivals(1)
-
     wait_bytes(b_in.at[pl.ds(0, plan.pole - 1)], recv_b)
     mixed = b_in[...].reshape(n, plan.rows)
     w = coordinates(dims, r)

time: 34.6 us -> 34 us (0.983)
  Pallas kernels: 33.9 us -> 33.2 us
    pallas_call x1, Pallas kernels: 33.1 us -> 32.4 us  [run_kernel(): pl.pallas_call(functools.partial(fused_kernel, plan), out_shape=(pltpu.VM...]
where the time goes in v5:
time: 34 us; the launch traced here: 33.9 us
  Pallas kernels  33.2 us (98%)
  between operations  0.66 us (2%)
    pallas_call x1, Pallas kernels, run_kernel(): pl.pallas_call(functools.partial(fused_kernel, plan), out_shape=(pltpu.VM...  32.4 us
    pallas_call x1, Pallas kernels, finish(): pl.pallas_call(finish_kernel, out_shape=(pltpu.HBM(panel.shape, F32), plt...  0.81 us

profile of v5, /device:TPU:1, one launch (start us, length us, event | category | flops | bytes accessed | tf_op | source)
XLA Modules:
  0.0 33.9 jit_solution(6991013292068233271)
XLA Ops:
  0.6 0.0 copy-start
  0.6 32.4 %fused.1 = (f32[128,256]{1,0:T(8,128)S(1)}, f32[800,120]{1,0:T(8,128)S(1)}) custom-call(s32[1,256]{1,0:T(1,128)} %bitcast.6, bf16[128,3072]{1,0:T(8,128)(2,1)} %refs_1_.1, bf16[128,256]{1,0:T(8,128)(2,1)} %refs_2_.1, s32[256,128]{1,0:T(8,128)} %bitcast.5, bf16[800,120]{1,0:T(8,128)(2,1)} %refs_4_.1), custom_call_target="tpu_custom_call" | custom-call | tf_op jit(solution)/shard_map/fused/pallas_call | solution.py:494
  33.1 0.0 copy-done
  33.1 0.8 %finish.1 = (f32[128,256]{1,0:T(8,128)}, f32[800,120]{1,0:T(8,128)}) custom-call(f32[128,256]{1,0:T(8,128)S(1)} %copy-done, f32[128,256]{1,0:T(8,128)S(1)} %get-tuple-element.6.product, f32[800,120]{1,0:T(8,128)S(1)} %get-tuple-element.7.flipped), custom_call_target="tpu_custom_call" | custom-call | tf_op jit(solution)/shard_map/finish/pallas_call | solution.py:523
Async XLA Ops:
  0.6 32.4 %copy-start = (f32[128,256]{1,0:T(8,128)S(1)}, f32[128,256]{1,0:T(8,128)}, u32[]{:S(2)}) copy-start(f32[128,256]{1,0:T(8,128)} %panel.1) | copy-start | bytes 393220
